TPU v7x, 32 devices: a whole 2x2x4 slice. The times are simulated.
32 devices in a mesh: dp: 2 (over x), tp: 16 (over y, z, core).
Axes of the slice: x: 2, y: 2, z: 4, core: 2. Of those that a mesh axis runs over, the one named last changes fastest.
Arguments:
- x: bfloat16 [128, 8192], P('dp'), parts along dimension 0
- k_cache: bfloat16 [128, 1024, 64, 128], P('dp', None, 'tp'), parts along dimension 0
- v_cache: bfloat16 [128, 1024, 64, 128], P('dp', None, 'tp'), parts along dimension 0
- gain_a: bfloat16 [8192], replicated
- wq: bfloat16 [8192, 8192], P(None, 'tp')
- wo: bfloat16 [8192, 8192], P('tp')
- gain_m: bfloat16 [8192], replicated
- w_gate: bfloat16 [8192, 24576], P(None, 'tp')
- w_up: bfloat16 [8192, 24576], P(None, 'tp')
- w_down: bfloat16 [24576, 8192], P('tp')
Outputs:
- output: bfloat16 [128, 8192], P('dp'), parts along dimension 0
There are 2 independent parts. A program takes and returns all parts, laid end to end along the dimension named above; an argument that names none is the same for every part.
All inputs are finite; a program needn't handle non-finite values.
Results may differ from a plain program's by a relative error of at most 0.017.
Values are sent between devices in bfloat16 or wider.
A program may use at most 2 GiB of HBM per device.

v0:
```python
import jax
import jax.numpy as jnp
from jax import lax
from jax.sharding import PartitionSpec as P

HEAD = 128
THETA = 10000


def normed(x, gain):
    wide = x.astype(jnp.float32)
    scale = lax.rsqrt(jnp.mean(wide * wide, -1, keepdims=True) + 1e-6)
    return (wide * scale * gain.astype(jnp.float32)).astype(jnp.bfloat16)


def turned(t, place, theta):
    half = t.shape[-1] // 2
    angle = place.astype(jnp.float32)[:, None] * theta ** (-jnp.arange(half, dtype=jnp.float32) / half)
    cos, sin = jnp.cos(angle)[:, None], jnp.sin(angle)[:, None]
    a, b = t[..., :half].astype(jnp.float32), t[..., half:].astype(jnp.float32)
    return jnp.concatenate([a * cos - b * sin, b * cos + a * sin], -1).astype(jnp.bfloat16)


def matmul(a, w):
    return jnp.dot(a, w, preferred_element_type=jnp.float32).astype(jnp.bfloat16)


def einsum(form, a, b):
    return jnp.einsum(form, a.astype(jnp.float32), b.astype(jnp.float32))


def seen_by(a, wq, k_cache, v_cache, head, theta):
    batch, cache, kv_heads = k_cache.shape[:3]
    place = jnp.full((batch,), cache - 1)
    q = turned(matmul(a, wq).reshape(batch, -1, head), place, theta).reshape(batch, kv_heads, -1, head)
    scores = einsum("bgsd,bugd->bgsu", q, k_cache) * head**-0.5
    weights = jax.nn.softmax(scores, -1).astype(jnp.bfloat16)
    return einsum("bgsu,bugd->bgsd", weights, v_cache).astype(jnp.bfloat16).reshape(batch, -1)


def hidden_of(b, w_gate, w_up):
    gate = jnp.dot(b, w_gate, preferred_element_type=jnp.float32)
    up = jnp.dot(b, w_up, preferred_element_type=jnp.float32)
    return (jax.nn.silu(gate) * up).astype(jnp.bfloat16)


def solution(mesh):
    def added(t, term):
        return (t.astype(jnp.float32) + lax.psum(term.astype(jnp.bfloat16), "tp").astype(jnp.float32)).astype(jnp.bfloat16)

    def step(x, k_cache, v_cache, gain_a, wq, wo, gain_m, w_gate, w_up, w_down):
        seen = seen_by(normed(x, gain_a), wq, k_cache, v_cache, HEAD, THETA)
        h = added(x, jnp.dot(seen, wo, preferred_element_type=jnp.float32))
        return added(h, jnp.dot(hidden_of(normed(h, gain_m), w_gate, w_up), w_down, preferred_element_type=jnp.float32))

    states, cache, columns, rows_of = P("dp", None), P("dp", None, "tp", None), P(None, "tp"), P("tp", None)
    return jax.shard_map(
        step,
        mesh=mesh,
        in_specs=(states, cache, cache, P(None), columns, rows_of, P(None), columns, columns, rows_of),
        out_specs=states,
        check_vma=False,
    )
```

profile of v0, /device:TPU:0, one launch (start us, length us, event | category | flops | bytes accessed | tf_op | source)
XLA Modules:
  0.0 310.8 jit_solution(5156785484425537612)
XLA Ops:
  6.5 0.0 all-reduce.3.cloned.1.call-start
  6.6 1.5 fusion.7
  8.1 0.7 convert_element_type.66
  8.9 5.3 %convolution_convert_fusion.2 = bf16[64,512]{1,0:T(8,128)(2,1)S(1)} fusion(bf16[8192,512]{1,0:T(8,128)(2,1)} %param.14, bf16[64,8192]{1,0:T(8,128)(2,1)} %param.10, f32[8192]{0:T(1024)S(1)} %convert_element_type.66, f32[64]{0:T(128)S(1)} %add_rsqrt_fusion.1), kind=kOutput, calls=%fused_computation.29 | convolution fusion | flops 539000832 | bytes 9535744 | tf_op jit(solution)/shard_map/dot_general | solution.py:25
  14.2 0.1 fusion.51
  14.4 0.1 maximum_bitcast_fusion
  14.5 30.6 %fusion.4 = f32[64,4,1,1024]{3,2,1,0:T(1,128)S(1)} fusion(bf16[64,1024,4,128]{3,2,1,0:T(4,128)(2,1)} %param.11, bf16[64,4,128,1]{2,0,1,3:T(8,128)(2,1)S(1)} %maximum_bitcast_fusion), kind=kOutput, calls=%fused_computation.4 | convolution fusion | flops 67108864 | bytes 68222976 | tf_op jit(solution)/shard_map/bgsd,bugd->bgsu/dot_general | solution.py:29
  45.1 1.4 fusion.19
  46.5 25.7 %fusion.2 = f32[64,4,1,128]{3,2,1,0:T(1,128)S(1)} fusion(bf16[64,1024,4,128]{3,2,1,0:T(4,128)(2,1)} %param.12, bf16[64,4,1024,1]{2,0,1,3:T(8,128)(2,1)S(1)} %fusion.19), kind=kOutput, calls=%fused_computation.2 | convolution fusion | flops 67108864 | bytes 67764224 | tf_op jit(solution)/shard_map/bgsu,bugd->bgsd/dot_general | solution.py:29
  72.2 0.0 copy-start.1
  72.3 0.0 copy-start
  72.3 6.0 %convolution_convert_fusion.1 = bf16[64,8192]{1,0:T(8,128)(2,1)} fusion(bf16[512,8192]{1,0:T(8,128)(2,1)} %param.15, bf16[8,8,4,128]{3,2,1,0:T(4,128)(2,1)S(1)} %bitcast.22), kind=kOutput, calls=%fused_computation.7 | convolution fusion | flops 537395200 | bytes 9502720 | tf_op jit(solution)/shard_map/dot_general | solution.py:53
  78.3 0.0 all-reduce.3.cloned.1.call-update
  78.3 0.0 all-reduce.5.cloned.1.call-start
  78.4 0.0 copy-done.1
  78.4 96.3 %all-reduce.3.cloned.1.call-done = bf16[64,8192]{1,0:T(8,128)(2,1)} async-done(((bf16[64,8192]{1,0:T(8,128)(2,1)}), bf16[64,8192]{1,0:T(8,128)(2,1)}) %all-reduce.3.cloned.1.call-update) | async-done | bytes 1048592 | tf_op jit(solution)/shard_map/psum | solution.py:49
  174.7 0.0 copy-done
  174.7 1.7 fusion.11
  176.4 10.5 %fusion.33 = f32[64,1536]{1,0:T(8,128)S(1)} fusion(bf16[8192,1536]{1,0:T(8,128)(2,1)} %param.17, bf16[64,8192]{1,0:T(8,128)(2,1)S(1)} %get-tuple-element.6, f32[8192]{0:T(1024)S(1)} %convert_element_type.77, f32[64]{0:T(128)S(1)} %add_rsqrt_fusion), kind=kOutput, calls=%fused_computation.41 | convolution fusion | flops 1612709888 | bytes 26640640 | tf_op jit(solution)/shard_map/dot_general | solution.py:42
  187.0 21.8 %convolution_convert_fusion = bf16[64,8192]{1,0:T(8,128)(2,1)} fusion(bf16[1536,8192]{1,0:T(8,128)(2,1)} %param.19, bf16[8192,1536]{1,0:T(8,128)(2,1)} %param.18, f32[64,1536]{1,0:T(8,128)S(1)} %fusion.33, bf16[64,8192]{1,0:T(8,128)(2,1)S(1)} %get-tuple-element.6, f32[8192]{0:T(1024)S(1)} %convert_element_type.77, f32[64]{0:T(128)S(1)} %add_rsqrt_fusion), kind=kOutput, calls=%fused_computation.6 | convolution fusion | flops 3224436736 | bytes 52855040 | tf_op jit(solution)/shard_map/dot_general | solution.py:54
  208.8 0.0 all-reduce.5.cloned.1.call-update
  208.8 92.7 %all-reduce.5.cloned.1.call-done = bf16[64,8192]{1,0:T(8,128)(2,1)} async-done(((bf16[64,8192]{1,0:T(8,128)(2,1)}), bf16[64,8192]{1,0:T(8,128)(2,1)}) %all-reduce.5.cloned.1.call-update) | async-done | bytes 1048592 | tf_op jit(solution)/shard_map/psum | solution.py:49
  301.5 2.4 fusion.14
  (7 shorter events, 0.2 us)
Async XLA Ops:
  6.5 168.2 %all-reduce.3.cloned.1.call-start = ((), (), s32[]{:S(2)}) async-start(), calls=%async_computation | async-start | bytes 2097152 | tf_op jit(solution)/shard_map/psum | solution.py:49
  72.2 6.1 %copy-start.1 = (bf16[8192]{0:T(1024)(128)(2,1)S(1)}, bf16[8192]{0:T(1024)(128)(2,1)}, u32[]{:S(2)}) copy-start(bf16[8192]{0:T(1024)(128)(2,1)} %param.16) | copy-start | bytes 49156
  72.3 102.5 %copy-start = (bf16[64,8192]{1,0:T(8,128)(2,1)S(1)}, bf16[64,8192]{1,0:T(8,128)(2,1)}, u32[]{:S(2)}) copy-start(bf16[64,8192]{1,0:T(8,128)(2,1)} %param.10) | copy-start | bytes 3145732
  78.3 223.2 %all-reduce.5.cloned.1.call-start = ((), (), s32[]{:S(2)}) async-start(), calls=%async_computation.1 | async-start | bytes 2097152 | tf_op jit(solution)/shard_map/psum | solution.py:49
Sparse Core Ops, SparseCore 0:
  78.5 96.2 all-reduce.2
  208.9 92.5 all-reduce.4
where the time goes:
time: 311 us
  waiting for transfers between devices  189 us (61%)
  matrix products  100 us (32%)
  between operations  13.5 us (4%)
  other arithmetic  8.04 us (3%)
    psum x2, waiting for transfers between devices, added(): lax.psum(term.astype(jnp.bfloat16), 'tp').astype(jnp.float32)  189 us
    dot_general x2, matrix products, einsum(): return jnp.einsum(form, a.astype(jnp.float32), b.astype(jnp.float32))  56.3 us
    dot_general x1, matrix products, step(): jnp.dot(hidden_of(normed(h, gain_m), w_gate, w_up), w_down, preferred_ele...  21.8 us
    dot_general x1, matrix products, hidden_of(): gate = jnp.dot(b, w_gate, preferred_element_type=jnp.float32)  10.5 us
  transfers between devices with their start and end apart: 2, of which 2 were waited for; matrix products, arithmetic and copies ran while one was open for 0% of the time, Pallas kernels for 0%

commit v1 on v0

v1 whole, which is shorter than its diff:
```python
import jax
import jax.numpy as jnp
from jax import lax
from jax.experimental import pallas as pl
from jax.experimental.pallas import tpu as pltpu
from jax.sharding import PartitionSpec as P

HEAD = 128
THETA = 10000
F32 = jnp.float32
BF = jnp.bfloat16
GROUP = 4
SLOTS = 12


def normed(x, gain):
    wide = x.astype(jnp.float32)
    scale = lax.rsqrt(jnp.mean(wide * wide, -1, keepdims=True) + 1e-6)
    return (wide * scale * gain.astype(jnp.float32)).astype(jnp.bfloat16)


def turned(t, place, theta):
    half = t.shape[-1] // 2
    angle = place.astype(jnp.float32)[:, None] * theta ** (-jnp.arange(half, dtype=jnp.float32) / half)
    cos, sin = jnp.cos(angle)[:, None], jnp.sin(angle)[:, None]
    a, b = t[..., :half].astype(jnp.float32), t[..., half:].astype(jnp.float32)
    return jnp.concatenate([a * cos - b * sin, b * cos + a * sin], -1).astype(jnp.bfloat16)


def matmul(a, w):
    return jnp.dot(a, w, preferred_element_type=jnp.float32).astype(jnp.bfloat16)


def scores_of(q, k_ref):
    rows = k_ref.shape[0] // 2
    both = jnp.concatenate([k_ref[0:rows, :], k_ref[rows : 2 * rows, :]], axis=1)
    return lax.dot_general(q, both, (((1,), (1,)), ((), ())), preferred_element_type=F32)


def weights_of(s):
    row, lane = lax.broadcasted_iota(jnp.int32, s.shape, 0), lax.broadcasted_iota(jnp.int32, s.shape, 1)
    s = jnp.where((row & 3) == (lane & 3), s * HEAD**-0.5, -jnp.inf)
    top = jnp.max(s, axis=1, keepdims=True)
    top = jnp.maximum(top, jnp.concatenate([top[4:], top[:4]], 0))
    e = jnp.exp(s - top)
    total = jnp.sum(e, axis=1, keepdims=True)
    total = total + jnp.concatenate([total[4:], total[:4]], 0)
    return (e * (1.0 / total)).astype(BF)


def mixed(p, v_ref):
    rows = v_ref.shape[0] // 2
    both = jnp.concatenate([v_ref[0:rows, :], v_ref[rows : 2 * rows, :]], axis=1)
    o = jnp.dot(p, both, preferred_element_type=F32)
    return o[0:4, 0:HEAD] + o[4:8, HEAD : 2 * HEAD]


def attention_kernel(q_ref, k_hbm, v_hbm, o_ref, kb, vb, sb, k_sem, v_sem):
    batch = k_hbm.shape[0]
    steps = batch // GROUP

    def k_copy(b):
        slot = lax.rem(b, SLOTS)
        return pltpu.make_async_copy(k_hbm.at[b], kb.at[slot], k_sem.at[slot])

    def v_copy(b):
        slot = lax.rem(b, SLOTS)
        return pltpu.make_async_copy(v_hbm.at[b], vb.at[slot], v_sem.at[slot])

    def first(b, carry):
        k_copy(b).start()
        v_copy(b).start()
        return carry

    lax.fori_loop(0, SLOTS, first, 0)

    def wait(copy, t):
        for j in range(GROUP):
            copy(t * GROUP + j).wait()

    def refill(copy, t):
        for j in range(GROUP):
            b = t * GROUP + j

            @pl.when(b + SLOTS < batch)
            def _():
                copy(b + SLOTS).start()

    def score(t):
        for j in range(GROUP):
            b = t * GROUP + j
            sb[lax.rem(t, 2), j] = scores_of(q_ref[b].astype(BF), kb.at[lax.rem(b, SLOTS)])

    def mix(t):
        ps = [weights_of(sb[lax.rem(t, 2), j]) for j in range(GROUP)]
        for j in range(GROUP):
            b = t * GROUP + j
            o_ref[b] = mixed(ps[j], vb.at[lax.rem(b, SLOTS)])

    wait(k_copy, 0)
    score(0)

    def body(t, carry):
        wait(v_copy, t)
        wait(k_copy, t + 1)
        refill(k_copy, t)
        score(t + 1)
        mix(t)
        refill(v_copy, t)
        return carry

    lax.fori_loop(0, steps - 1, body, 0)
    wait(v_copy, steps - 1)
    mix(steps - 1)


def attention(q, k, v):
    batch, rows = k.shape[:2]
    q = q.astype(F32)
    none = jnp.zeros_like(q)
    q = jnp.concatenate([jnp.concatenate([q, none], 2), jnp.concatenate([none, q], 2)], 1)
    return pl.pallas_call(
        attention_kernel,
        out_shape=jax.ShapeDtypeStruct((batch, 4, HEAD), F32),
        in_specs=[pl.BlockSpec(memory_space=pltpu.VMEM)] + [pl.BlockSpec(memory_space=pl.ANY)] * 2,
        out_specs=pl.BlockSpec(memory_space=pltpu.VMEM),
        scratch_shapes=[
            pltpu.VMEM((SLOTS, rows, HEAD), BF),
            pltpu.VMEM((SLOTS, rows, HEAD), BF),
            pltpu.VMEM((2, GROUP, 8, rows // 2), F32),
            pltpu.SemaphoreType.DMA((SLOTS,)),
            pltpu.SemaphoreType.DMA((SLOTS,)),
        ],
        compiler_params=pltpu.CompilerParams(vmem_limit_bytes=56 * 2**20),
        name="attention",
    )(q, k, v)


CHIPS = 8


def added_kernel(term, t_ref, out_ref, near, mine, parts, whole, near_sem, part_sem, back_sem, pass_sem):
    me = lax.axis_index("tp")
    core, chip = lax.rem(me, 2), me // 2
    twin = chip * 2 + (1 - core)
    width = term.shape[1] // (2 * CHIPS)
    half = width * CHIPS

    def peer(d):
        return lax.rem(chip + d, CHIPS)

    def columns(o, w):
        return pl.ds(pl.multiple_of(o * w, w), w)

    def copy(src, dst, sems, i, device):
        return pltpu.make_async_remote_copy(
            src_ref=src, dst_ref=dst, send_sem=sems.at[0, i], recv_sem=sems.at[1, i],
            device_id={"tp": device}, device_id_type=pl.DeviceIdType.MESH,
        )

    barrier = pltpu.get_barrier_semaphore()
    pl.semaphore_signal(barrier, inc=1, device_id={"tp": twin}, device_id_type=pl.DeviceIdType.MESH)
    for d in range(1, CHIPS):
        pl.semaphore_signal(barrier, inc=1, device_id={"tp": peer(d) * 2 + core}, device_id_type=pl.DeviceIdType.MESH)
    pl.semaphore_wait(barrier, CHIPS)

    over = copy(term.at[:, columns(1 - core, half)], near, near_sem, 0, twin)
    over.start()
    over.wait()
    mine[...] = (term[:, columns(core, half)].astype(F32) + near[...].astype(F32)).astype(BF)
    out = []
    for d in range(1, CHIPS):
        c = copy(mine.at[:, columns(peer(d), width)], parts.at[d], part_sem, d, peer(d) * 2 + core)
        c.start()
        out.append(c)
    own = core * CHIPS + chip
    total = term[:, columns(own, width)].astype(F32) + near[:, columns(chip, width)].astype(F32)
    for c in out:
        c.wait()
    for d in range(1, CHIPS):
        total = total + parts[d].astype(F32)
    whole[:, columns(own, width)] = (t_ref[:, columns(own, width)].astype(F32) + total).astype(BF)

    passed = copy(whole.at[:, columns(own, width)], whole.at[:, columns(own, width)], pass_sem, 0, twin)
    back = []
    for d in range(1, CHIPS):
        c = copy(whole.at[:, columns(own, width)], whole.at[:, columns(own, width)], back_sem, d, peer(d) * 2 + core)
        c.start()
        back.append(c)
    passed.start()
    on = [passed]
    for d in range(1, CHIPS):
        back[d - 1].wait_recv()
        block = columns(core * CHIPS + lax.rem(chip + CHIPS - d, CHIPS), width)
        c = copy(whole.at[:, block], whole.at[:, block], pass_sem, d, twin)
        c.start()
        on.append(c)
    for c in back:
        c.wait_send()
    for c in on:
        c.wait()
    out_ref[...] = whole[...]


def added(t, term, number):
    rows, d = t.shape
    width = d // (2 * CHIPS)
    return pl.pallas_call(
        added_kernel,
        out_shape=jax.ShapeDtypeStruct((rows, d), BF),
        in_specs=[pl.BlockSpec(memory_space=pltpu.VMEM)] * 2,
        out_specs=pl.BlockSpec(memory_space=pltpu.VMEM),
        scratch_shapes=[
            pltpu.VMEM((rows, d // 2), BF),
            pltpu.VMEM((rows, d // 2), BF),
            pltpu.VMEM((CHIPS, rows, width), BF),
            pltpu.VMEM((rows, d), BF),
            pltpu.SemaphoreType.DMA((2, 1)),
            pltpu.SemaphoreType.DMA((2, CHIPS)),
            pltpu.SemaphoreType.DMA((2, CHIPS)),
            pltpu.SemaphoreType.DMA((2, CHIPS)),
        ],
        compiler_params=pltpu.CompilerParams(collective_id=number, has_side_effects=True, vmem_limit_bytes=16 * 2**20),
        name=f"added_{number}",
    )(term.astype(BF), t)


def hidden_of(b, w_gate, w_up):
    gate = jnp.dot(b, w_gate, preferred_element_type=jnp.float32)
    up = jnp.dot(b, w_up, preferred_element_type=jnp.float32)
    return (jax.nn.silu(gate) * up).astype(jnp.bfloat16)


def solution(mesh):
    def step(x, k_cache, v_cache, gain_a, wq, wo, gain_m, w_gate, w_up, w_down):
        batch, cache, heads = k_cache.shape[:3]
        place = jnp.full((batch,), cache - 1)
        q = turned(matmul(normed(x, gain_a), wq).reshape(batch, heads, HEAD), place, THETA)
        seen = attention(q, k_cache.reshape(batch, cache * heads, HEAD), v_cache.reshape(batch, cache * heads, HEAD))
        seen = seen.astype(BF).reshape(batch, heads * HEAD)
        h = added(x, jnp.dot(seen, wo, preferred_element_type=jnp.float32), 0)
        hidden = hidden_of(normed(h, gain_m), w_gate, w_up)
        return added(h, jnp.dot(hidden, w_down, preferred_element_type=jnp.float32), 1)

    states, cache, columns, rows_of = P("dp", None), P("dp", None, "tp", None), P(None, "tp"), P("tp", None)
    return jax.shard_map(
        step,
        mesh=mesh,
        in_specs=(states, cache, cache, P(None), columns, rows_of, P(None), columns, columns, rows_of),
        out_specs=states,
        check_vma=False,
    )
```

time: 311 us -> 159 us (0.51)
  waiting for transfers between devices: 189 us -> 0 us
  Pallas kernels: 0 us -> 110 us
  matrix products: 100 us -> 41.7 us
  between operations: 13.5 us -> 0.11 us
    psum x2 -> x0, waiting for transfers between devices: 189 us -> none  [added(): lax.psum(term.astype(jnp.bfloat16), 'tp').astype(jnp.float32)]
    pallas_call x0 -> x3, Pallas kernels: none -> 110 us  [the longest x2 66.7 us: added(): pl.pallas_call(added_kernel, out_shape=jax.ShapeDtypeStruct((rows, d), BF...]
    dot_general x4 -> x2, matrix products: 84.1 us -> 25.8 us  [the longest x1 20.9 us: step(): jnp.dot(hidden, w_down, preferred_element_type=jnp.float32)]
  transfers between devices with their start and end apart: 2 -> 0, of which waited for: 2 -> 0; matrix products, arithmetic and copies ran while one was open for 0% -> 0% of each run, Pallas kernels for 0% -> 0%
where the time goes in v1:
time: 159 us; the launch traced here: 158 us
  Pallas kernels  110 us (69%)
  matrix products  41.7 us (26%)
  other arithmetic  5.48 us (3%)
    pallas_call x2, Pallas kernels, added(): pl.pallas_call(added_kernel, out_shape=jax.ShapeDtypeStruct((rows, d), BF...  66.7 us
    pallas_call x1, Pallas kernels, attention(): pl.pallas_call(attention_kernel, out_shape=jax.ShapeDtypeStruct((batch, 4...  43.2 us
    dot_general x1, matrix products, step(): jnp.dot(hidden, w_down, preferred_element_type=jnp.float32)  20.9 us
    dot_general x1, matrix products, hidden_of(): gate = jnp.dot(b, w_gate, preferred_element_type=jnp.float32)  10.5 us
    dot_general x1, matrix products, matmul(): jnp.dot(a, w, preferred_element_type=jnp.float32).astype(jnp.bfloat16)  5.34 us
    dot_general x1, matrix products, step(): h = added(x, jnp.dot(seen, wo, preferred_element_type=jnp.float32), 0)  4.95 us

profile of v1, /device:TPU:0, one launch (start us, length us, event | category | flops | bytes accessed | tf_op | source)
XLA Modules:
  0.0 158.2 jit_solution(7291876250880157249)
XLA Ops:
  0.0 1.5 fusion.1
  1.5 0.1 fusion.26
  1.6 0.7 convert_element_type.53
  2.3 0.7 convert_element_type.44
  3.1 5.3 %convolution_convert_fusion.2 = bf16[64,512]{1,0:T(8,128)(2,1)S(1)} fusion(bf16[8192,512]{1,0:T(8,128)(2,1)} %param.14, bf16[64,8192]{1,0:T(8,128)(2,1)} %t_ref.1, f32[8192]{0:T(1024)S(1)} %convert_element_type.44, f32[64]{0:T(128)S(1)} %add_rsqrt_fusion.1), kind=kOutput, calls=%fused_computation.14 | convolution fusion | flops 539000832 | bytes 9535744 | tf_op jit(solution)/shard_map/dot_general | solution.py:31
  8.4 0.1 fusion.21
  8.6 0.1 maximum_convert_fusion
  8.7 0.9 select_maximum_fusion.q_ref
  9.6 43.2 %attention.1 = f32[64,4,128]{2,1,0:T(4,128)} custom-call(f32[64,8,256]{2,1,0:T(8,128)} %select_maximum_fusion.q_ref, bf16[64,4096,128]{2,1,0:T(8,128)(2,1)} %bitcast.k_hbm, bf16[64,4096,128]{2,1,0:T(8,128)(2,1)} %bitcast.1.v_hbm), custom_call_target="tpu_custom_call" | custom-call | tf_op jit(solution)/shard_map/attention/pallas_call | solution.py:122
  52.8 0.0 copy-start
  52.8 1.0 convert_element_type.50
  53.8 5.0 %convolution_convert_fusion.1.term = bf16[64,8192]{1,0:T(8,128)(2,1)S(1)} fusion(bf16[512,8192]{1,0:T(8,128)(2,1)} %param.15, bf16[8,8,4,128]{3,2,1,0:T(4,128)(2,1)S(1)} %bitcast.11), kind=kOutput, calls=%fused_computation.1 | convolution fusion | flops 537395200 | bytes 9502720 | tf_op jit(solution)/shard_map/dot_general | solution.py:241
  58.8 0.0 copy-done
  58.8 33.9 %added_0.1.t_ref = bf16[64,8192]{1,0:T(8,128)(2,1)S(1)} custom-call(bf16[64,8192]{1,0:T(8,128)(2,1)S(1)} %convolution_convert_fusion.1.term, bf16[64,8192]{1,0:T(8,128)(2,1)S(1)} %copy-done), custom_call_target="tpu_custom_call" | custom-call | tf_op jit(solution)/shard_map/added_0/pallas_call | solution.py:208
  92.7 0.3 fusion.4
  93.1 10.5 %fusion.17 = f32[64,1536]{1,0:T(8,128)S(1)} fusion(bf16[8192,1536]{1,0:T(8,128)(2,1)} %param.17, bf16[64,8192]{1,0:T(8,128)(2,1)S(1)} %added_0.1.t_ref, f32[8192]{0:T(1024)S(1)} %convert_element_type.53, f32[64]{0:T(128)S(1)} %add_rsqrt_fusion), kind=kOutput, calls=%fused_computation.25 | convolution fusion | flops 1612709888 | bytes 26640640 | tf_op jit(solution)/shard_map/dot_general | solution.py:229
  103.6 20.9 %convolution_convert_fusion.term = bf16[64,8192]{1,0:T(8,128)(2,1)S(1)} fusion(bf16[1536,8192]{1,0:T(8,128)(2,1)} %param.19, bf16[8192,1536]{1,0:T(8,128)(2,1)} %param.18, f32[64,1536]{1,0:T(8,128)S(1)} %fusion.17, bf16[64,8192]{1,0:T(8,128)(2,1)S(1)} %added_0.1.t_ref, f32[8192]{0:T(1024)S(1)} %convert_element_type.53, f32[64]{0:T(128)S(1)} %add_rsqrt_fusion), kind=kOutput, calls=%fused_computation | convolution fusion | flops 3224436736 | bytes 52855040 | tf_op jit(solution)/shard_map/dot_general | solution.py:243
  124.4 32.8 %added_1.1 = bf16[64,8192]{1,0:T(8,128)(2,1)S(1)} custom-call(bf16[64,8192]{1,0:T(8,128)(2,1)S(1)} %convolution_convert_fusion.term, bf16[64,8192]{1,0:T(8,128)(2,1)S(1)} %added_0.1.t_ref), custom_call_target="tpu_custom_call" | custom-call | tf_op jit(solution)/shard_map/added_1/pallas_call | solution.py:208
  157.2 1.0 copy.17
  (3 shorter events, 0.0 us)
Async XLA Ops:
  52.8 6.0 %copy-start = (bf16[64,8192]{1,0:T(8,128)(2,1)S(1)}, bf16[64,8192]{1,0:T(8,128)(2,1)}, u32[]{:S(2)}) copy-start(bf16[64,8192]{1,0:T(8,128)(2,1)} %t_ref.1) | copy-start | bytes 3145732

commit v2 on v1

--- a/solution.py
+++ b/solution.py
@@ -139,7 +139,7 @@
 CHIPS = 8
 
 
-def added_kernel(term, t_ref, out_ref, near, mine, parts, whole, near_sem, part_sem, back_sem, pass_sem):
+def exchanged(term, t_ref, near, mine, parts, whole, near_sem, part_sem, back_sem, pass_sem):
     me = lax.axis_index("tp")
     core, chip = lax.rem(me, 2), me // 2
     twin = chip * 2 + (1 - core)
@@ -199,36 +199,140 @@
         c.wait_send()
     for c in on:
         c.wait()
+
+
+def added_kernel(term, t_ref, out_ref, near, mine, parts, whole, *sems):
+    exchanged(term, t_ref, near, mine, parts, whole, *sems)
     out_ref[...] = whole[...]
+
+
+def scratch_of(rows, d):
+    width = d // (2 * CHIPS)
+    return [
+        pltpu.VMEM((rows, d // 2), BF),
+        pltpu.VMEM((rows, d // 2), BF),
+        pltpu.VMEM((CHIPS, rows, width), BF),
+        pltpu.VMEM((rows, d), BF),
+        pltpu.SemaphoreType.DMA((2, 1)),
+        pltpu.SemaphoreType.DMA((2, CHIPS)),
+        pltpu.SemaphoreType.DMA((2, CHIPS)),
+        pltpu.SemaphoreType.DMA((2, CHIPS)),
+    ]
 
 
 def added(t, term, number):
     rows, d = t.shape
-    width = d // (2 * CHIPS)
     return pl.pallas_call(
         added_kernel,
         out_shape=jax.ShapeDtypeStruct((rows, d), BF),
         in_specs=[pl.BlockSpec(memory_space=pltpu.VMEM)] * 2,
         out_specs=pl.BlockSpec(memory_space=pltpu.VMEM),
-        scratch_shapes=[
-            pltpu.VMEM((rows, d // 2), BF),
-            pltpu.VMEM((rows, d // 2), BF),
-            pltpu.VMEM((CHIPS, rows, width), BF),
-            pltpu.VMEM((rows, d), BF),
-            pltpu.SemaphoreType.DMA((2, 1)),
-            pltpu.SemaphoreType.DMA((2, CHIPS)),
-            pltpu.SemaphoreType.DMA((2, CHIPS)),
-            pltpu.SemaphoreType.DMA((2, CHIPS)),
-        ],
+        scratch_shapes=scratch_of(rows, d),
         compiler_params=pltpu.CompilerParams(collective_id=number, has_side_effects=True, vmem_limit_bytes=16 * 2**20),
         name=f"added_{number}",
     )(term.astype(BF), t)
 
 
-def hidden_of(b, w_gate, w_up):
-    gate = jnp.dot(b, w_gate, preferred_element_type=jnp.float32)
-    up = jnp.dot(b, w_up, preferred_element_type=jnp.float32)
-    return (jax.nn.silu(gate) * up).astype(jnp.bfloat16)
+DEPTH = 1024
+PANEL = 1024
+AHEAD = 4
+PANELS = 5
+
+
+def second_kernel(term, t_ref, gain_ref, gate_hbm, up_hbm, down_hbm, h_ref, out_ref, gates, ups, downs, gate, up, w_sem, d_sem, near, mine, parts, whole, *sems):
+    d = t_ref.shape[1]
+    steps, panels = d // DEPTH, d // PANEL
+
+    def gate_copy(i):
+        slot = lax.rem(i, AHEAD)
+        return pltpu.make_async_copy(gate_hbm.at[pl.ds(pl.multiple_of(i * DEPTH, DEPTH), DEPTH), :], gates.at[slot], w_sem.at[0, slot])
+
+    def up_copy(i):
+        slot = lax.rem(i, AHEAD)
+        return pltpu.make_async_copy(up_hbm.at[pl.ds(pl.multiple_of(i * DEPTH, DEPTH), DEPTH), :], ups.at[slot], w_sem.at[1, slot])
+
+    def down_copy(i):
+        slot = lax.rem(i, PANELS)
+        return pltpu.make_async_copy(down_hbm.at[:, pl.ds(pl.multiple_of(i * PANEL, PANEL), PANEL)], downs.at[slot], d_sem.at[slot])
+
+    def first(i, carry):
+        gate_copy(i).start()
+        up_copy(i).start()
+        return carry
+
+    def first_down(i, carry):
+        down_copy(i).start()
+        return carry
+
+    lax.fori_loop(0, AHEAD, first, 0)
+    lax.fori_loop(0, PANELS, first_down, 0)
+    exchanged(term, t_ref, near, mine, parts, whole, *sems)
+
+    def piece(i):
+        return pl.ds(pl.multiple_of(i * DEPTH, DEPTH), DEPTH)
+
+    def squares(i, total):
+        wide = whole[:, piece(i)].astype(F32)
+        h_ref[:, piece(i)] = whole[:, piece(i)]
+        return total + jnp.sum(wide * wide, -1, keepdims=True)
+
+    square = lax.fori_loop(0, steps, squares, jnp.zeros((t_ref.shape[0], 1), F32))
+    scale = lax.rsqrt(square / d + 1e-6)
+    gate[...] = jnp.zeros_like(gate)
+    up[...] = jnp.zeros_like(up)
+
+    def body(i, carry):
+        slot = lax.rem(i, AHEAD)
+        b = (whole[:, piece(i)].astype(F32) * scale * gain_ref[:, piece(i)].astype(F32)).astype(BF)
+        gate_copy(i).wait()
+        up_copy(i).wait()
+        gate[...] += jnp.dot(b, gates[slot], preferred_element_type=F32)
+        up[...] += jnp.dot(b, ups[slot], preferred_element_type=F32)
+
+        @pl.when(i + AHEAD < steps)
+        def _():
+            gate_copy(i + AHEAD).start()
+            up_copy(i + AHEAD).start()
+
+        return carry
+
+    lax.fori_loop(0, steps, body, 0)
+    hidden = (jax.nn.silu(gate[...]) * up[...]).astype(BF)
+
+    def panel(i, carry):
+        down_copy(i).wait()
+        out_ref[:, pl.ds(pl.multiple_of(i * PANEL, PANEL), PANEL)] = jnp.dot(hidden, downs[lax.rem(i, PANELS)], preferred_element_type=F32).astype(BF)
+
+        @pl.when(i + PANELS < panels)
+        def _():
+            down_copy(i + PANELS).start()
+
+        return carry
+
+    lax.fori_loop(0, panels, panel, 0)
+
+
+def second(t, term, gain, w_gate, w_up, w_down):
+    rows, d = t.shape
+    units = w_gate.shape[1]
+    return pl.pallas_call(
+        second_kernel,
+        out_shape=[jax.ShapeDtypeStruct((rows, d), BF)] * 2,
+        in_specs=[pl.BlockSpec(memory_space=pltpu.VMEM)] * 3 + [pl.BlockSpec(memory_space=pl.ANY)] * 3,
+        out_specs=[pl.BlockSpec(memory_space=pltpu.VMEM)] * 2,
+        scratch_shapes=[
+            pltpu.VMEM((AHEAD, DEPTH, units), BF),
+            pltpu.VMEM((AHEAD, DEPTH, units), BF),
+            pltpu.VMEM((PANELS, units, PANEL), BF),
+            pltpu.VMEM((rows, units), F32),
+            pltpu.VMEM((rows, units), F32),
+            pltpu.SemaphoreType.DMA((2, AHEAD)),
+            pltpu.SemaphoreType.DMA((PANELS,)),
+        ]
+        + scratch_of(rows, d),
+        compiler_params=pltpu.CompilerParams(collective_id=0, has_side_effects=True, vmem_limit_bytes=58 * 2**20),
+        name="second",
+    )(term.astype(BF), t, gain.reshape(1, d), w_gate, w_up, w_down)
 
 
 def solution(mesh):
@@ -238,9 +342,8 @@
         q = turned(matmul(normed(x, gain_a), wq).reshape(batch, heads, HEAD), place, THETA)
         seen = attention(q, k_cache.reshape(batch, cache * heads, HEAD), v_cache.reshape(batch, cache * heads, HEAD))
         seen = seen.astype(BF).reshape(batch, heads * HEAD)
-        h = added(x, jnp.dot(seen, wo, preferred_element_type=jnp.float32), 0)
-        hidden = hidden_of(normed(h, gain_m), w_gate, w_up)
-        return added(h, jnp.dot(hidden, w_down, preferred_element_type=jnp.float32), 1)
+        h, term = second(x, jnp.dot(seen, wo, preferred_element_type=jnp.float32), gain_m, w_gate, w_up, w_down)
+        return added(h, term, 1)
 
     states, cache, columns, rows_of = P("dp", None), P("dp", None, "tp", None), P(None, "tp"), P("tp", None)
     return jax.shard_map(

time: 159 us -> 149 us (0.937)
  matrix products: 41.7 us -> 11.3 us
  Pallas kernels: 110 us -> 129 us
  local copies, waits for them, and re-layouts: 1 us -> 4.06 us
    pallas_call x0 -> x1, Pallas kernels: none -> 53 us  [second(): pl.pallas_call(second_kernel, out_shape=[jax.ShapeDtypeStruct((rows, d),...]
    pallas_call x2 -> x1, Pallas kernels: 66.7 us -> 32.8 us  [added(): pl.pallas_call(added_kernel, out_shape=jax.ShapeDtypeStruct((rows, d), BF...]
    dot_general x3 -> x1, matrix products: 36.3 us -> 5.93 us  [step(): jnp.dot(seen, wo, preferred_element_type=jnp.float32)]
    unnamed x3 -> x7, local copies, waits for them, and re-layouts: 0.98 us -> 3.42 us
where the time goes in v2:
time: 149 us
  Pallas kernels  129 us (87%)
  matrix products  11.3 us (8%)
  other arithmetic  4.36 us (3%)
  local copies, waits for them, and re-layouts  4.06 us (3%)
    pallas_call x1, Pallas kernels, second(): pl.pallas_call(second_kernel, out_shape=[jax.ShapeDtypeStruct((rows, d),...  53 us
    pallas_call x1, Pallas kernels, attention(): pl.pallas_call(attention_kernel, out_shape=jax.ShapeDtypeStruct((batch, 4...  43.2 us
    pallas_call x1, Pallas kernels, added(): pl.pallas_call(added_kernel, out_shape=jax.ShapeDtypeStruct((rows, d), BF...  32.8 us
    dot_general x1, matrix products, step(): jnp.dot(seen, wo, preferred_element_type=jnp.float32)  5.93 us
    dot_general x1, matrix products, matmul(): jnp.dot(a, w, preferred_element_type=jnp.float32).astype(jnp.bfloat16)  5.35 us
    unnamed x7, local copies, waits for them, and re-layouts  3.42 us

profile of v2, /device:TPU:0, one launch (start us, length us, event | category | flops | bytes accessed | tf_op | source)
XLA Modules:
  0.0 148.8 jit_solution(17089680336567935449)
XLA Ops:
  0.0 1.5 %fusion = f32[64]{0:T(128)S(1)} fusion(bf16[64,8192]{1,0:T(8,128)(2,1)} %t_ref.1), kind=kLoop, calls=%fused_computation.3 | loop fusion | flops 1572800 | bytes 1048832 | tf_op jit(solution)/shard_map/reduce_sum | solution.py:18
  1.5 0.1 fusion.12
  1.6 0.7 convert_element_type.29
  2.3 0.0 copy-start.2
  2.3 5.4 %convolution_convert_fusion.1 = bf16[64,512]{1,0:T(8,128)(2,1)S(1)} fusion(bf16[8192,512]{1,0:T(8,128)(2,1)} %param.14, bf16[64,8192]{1,0:T(8,128)(2,1)} %t_ref.1, f32[8192]{0:T(1024)S(1)} %convert_element_type.29, f32[64]{0:T(128)S(1)} %add_rsqrt_fusion), kind=kOutput, calls=%fused_computation.6 | convolution fusion | flops 539000832 | bytes 9535744 | tf_op jit(solution)/shard_map/dot_general | solution.py:31
  7.7 0.0 copy-done.2
  7.7 0.6 reshape.36.gain_ref
  8.4 0.1 fusion.7
  8.5 0.1 maximum_convert_fusion
  8.6 0.9 select_maximum_fusion.q_ref
  9.5 43.2 %attention.1 = f32[64,4,128]{2,1,0:T(4,128)} custom-call(f32[64,8,256]{2,1,0:T(8,128)} %select_maximum_fusion.q_ref, bf16[64,4096,128]{2,1,0:T(8,128)(2,1)} %bitcast.k_hbm, bf16[64,4096,128]{2,1,0:T(8,128)(2,1)} %bitcast.1.v_hbm), custom_call_target="tpu_custom_call" | custom-call | tf_op jit(solution)/shard_map/attention/pallas_call | solution.py:122
  52.7 0.9 convert_element_type.35
  53.6 5.9 %convolution_convert_fusion.term = bf16[64,8192]{1,0:T(8,128)(2,1)} fusion(bf16[512,8192]{1,0:T(8,128)(2,1)} %param.15, bf16[8,8,4,128]{3,2,1,0:T(4,128)(2,1)S(1)} %bitcast.8), kind=kOutput, calls=%fused_computation | convolution fusion | flops 537395200 | bytes 9502720 | tf_op jit(solution)/shard_map/dot_general | solution.py:345
  59.6 53.0 %second.1 = (bf16[64,8192]{1,0:T(8,128)(2,1)}, bf16[64,8192]{1,0:T(8,128)(2,1)}) custom-call(bf16[64,8192]{1,0:T(8,128)(2,1)} %convolution_convert_fusion.term, bf16[64,8192]{1,0:T(8,128)(2,1)} %t_ref.1, bf16[1,8192]{1,0:T(2,128)(2,1)} %reshape.36.gain_ref, bf16[8192,1536]{1,0:T(8,128)(2,1)} %gate_hbm.1, bf16[8192,1536]{1,0:T(8,128)(2,1)} %up_hbm.1, ...), custom_call_target="tpu_custom_call" | custom-call | tf_op jit(solution)/shard_map/second/pallas_call | solution.py:318
  112.6 0.0 copy-start
  112.6 1.2 copy-done
  113.8 0.0 copy-start.1
  113.8 1.2 copy-done.1
  115.0 32.8 %added_1.1 = bf16[64,8192]{1,0:T(8,128)(2,1)S(1)} custom-call(bf16[64,8192]{1,0:T(8,128)(2,1)S(1)} %copy-done.1, bf16[64,8192]{1,0:T(8,128)(2,1)S(1)} %copy-done), custom_call_target="tpu_custom_call" | custom-call | tf_op jit(solution)/shard_map/added_1/pallas_call | solution.py:225
  147.9 1.0 copy.17
  (2 shorter events, 0.0 us)
Async XLA Ops:
  2.3 5.4 %copy-start.2 = (bf16[8192]{0:T(1024)(128)(2,1)S(1)}, bf16[8192]{0:T(1024)(128)(2,1)}, u32[]{:S(2)}) copy-start(bf16[8192]{0:T(1024)(128)(2,1)} %param.16) | copy-start | bytes 49156
  112.6 1.2 copy-start
  113.8 1.2 copy-start.1
